TPU v7x, 32 devices: a whole 2x2x4 slice. The times are simulated.
32 devices in a mesh: lon: 8 (over y, x, core), lat: 4 (over z).
Axes of the slice: x: 2, y: 2, z: 4, core: 2. Of those that a mesh axis runs over, the one named last changes fastest.
Arguments:
- fields: bfloat16 [4, 128, 32, 1024], P(None, None, 'lat', 'lon'), may hold values from -12 to 12
- bracket: int32 [32, 32, 1024], P(None, 'lat', 'lon'), may hold values from 0 to 126, as said below
- fraction: bfloat16 [32, 32, 1024], P(None, 'lat', 'lon'), may hold values from 0 to 1
Outputs:
- on_pressure: bfloat16 [4, 32, 32, 1024], P(None, None, ('lat', 'lon'))
- zonal_mean: float32 [4, 32, 32], P(None, None, ('lat', 'lon'))
- meridional: float32 [4, 32, 32], P(None, None, ('lat', 'lon'))
Inputs may be any that keep to these rules, and one draw needn't show every extreme that they name: bracket[p, r, c] - min(p * 4, 112) lies in 0 to 14 for every column, and each of these offsets occurs.
All inputs are finite; a program needn't handle non-finite values.
Results may differ from a plain program's by a relative error of at most 0.0012.
Values may be sent and summed in bfloat16 or wider, within the bound.
No kernel may reach another device: no remote copies, remote signals or barrier semaphores. Data moves between devices by JAX's collectives and lax.ppermute only.
A program may use at most 128 MiB of HBM per device.

v0:
```python
import functools

import jax
import jax.numpy as jnp
from jax import lax
from jax.experimental import pallas as pl
from jax.experimental.pallas import tpu as pltpu
from jax.sharding import PartitionSpec as P

WINDOW = 16
SUBLANES = 8
bf16, f32 = jnp.bfloat16, jnp.float32
VMEM = pl.BlockSpec(memory_space=pltpu.VMEM)


def interpolate_kernel(fields, bracket, fraction, payload, flat, totals, *, levels):
    groups, variables = fields.shape[:2]
    plev = bracket.shape[1]
    pairs = variables * plev
    step = levels // plev

    def one_group(group):
        for p in range(plev):
            base = min(p * step, levels - WINDOW)
            offset = bracket[group, p] - base
            index = jnp.concatenate([(offset + 1) >> 1, offset >> 1], 0).astype(f32).astype(bf16)
            high = index >= bf16(4)
            index = jnp.where(high, index - bf16(4), index)
            mid = index >= bf16(2)
            index = jnp.where(mid, index - bf16(2), index)
            low = index >= bf16(1)
            is_odd = (offset & 1) == 1
            weight = fraction[group, p].astype(f32)
            weight = jnp.where(is_odd, -weight, weight)
            for v in range(variables):
                w = [fields[group, v, base // 2 + k] for k in range(WINDOW // 2)]
                w = [jnp.where(low, w[k + 1], w[k]) for k in (0, 2, 4, 6)]
                w = [jnp.where(mid, w[k + 1], w[k]) for k in (0, 2)]
                picked = jnp.where(high, w[1], w[0]).astype(f32)
                even, odd = picked[:SUBLANES], picked[SUBLANES:]
                value = jnp.where(is_odd, odd, even) + weight * (odd - even)
                flat[pl.ds(v * plev + p, SUBLANES, stride=pairs), :] = value
        ones = jnp.ones((SUBLANES, flat.shape[1]), bf16)
        sums = []
        for r in range(SUBLANES):
            block = flat[r * pairs : (r + 1) * pairs, :].astype(bf16)
            payload[group * SUBLANES + r, :pairs, :] = block
            total = lax.dot_general(ones, block, (((1,), (1,)), ((), ())), preferred_element_type=f32)
            sums.append(total[:1])
        totals[group] = jnp.concatenate(sums, 0)

    if groups == 1:
        one_group(0)
    else:
        pl.loop(0, groups)(one_group)
    sums = totals[...].reshape(groups * SUBLANES, pairs)
    main = sums.astype(bf16)
    both = jnp.concatenate([main, (sums - main.astype(f32)).astype(bf16)], 0)
    for r in range(groups * SUBLANES):
        payload[r, pairs:, :] = both


def interpolate(fields, bracket, fraction):
    variables, levels, rows, columns = fields.shape
    plev = bracket.shape[0]
    groups = rows // SUBLANES
    pairs = variables * plev
    assert rows % SUBLANES == 0 and levels % 2 == 0 and pairs == columns
    grouped = fields.reshape(variables, levels, groups, SUBLANES, columns).transpose(2, 0, 1, 3, 4)
    grouped = grouped.reshape(groups, variables, levels // 2, 2 * SUBLANES, columns)
    bracket = bracket.reshape(plev, groups, SUBLANES, columns).transpose(1, 0, 2, 3)
    fraction = fraction.reshape(plev, groups, SUBLANES, columns).transpose(1, 0, 2, 3)
    return pl.pallas_call(
        functools.partial(interpolate_kernel, levels=levels),
        out_shape=jax.ShapeDtypeStruct((rows, pairs + 2 * rows, columns), bf16),
        in_specs=[VMEM] * 3,
        out_specs=VMEM,
        scratch_shapes=[
            pltpu.VMEM((SUBLANES * pairs, columns), f32),
            pltpu.VMEM((groups, SUBLANES, pairs), f32),
        ],
        name="interpolate",
    )(grouped, bracket, fraction)


def lay_kernel(received, whole, sem):
    parts, _, columns = received.shape
    pairs = whole.shape[0]
    copies = [
        pltpu.make_async_copy(
            received.at[j, :pairs], whole.at[:, j * columns : (j + 1) * columns], sem.at[j]
        )
        for j in range(parts)
    ]
    for copy in copies:
        copy.start()
    for copy in copies:
        copy.wait()


def lay(received, pairs):
    parts, _, columns = received.shape
    return pl.pallas_call(
        lay_kernel,
        out_shape=jax.ShapeDtypeStruct((pairs, parts * columns), bf16),
        in_specs=[pl.BlockSpec(memory_space=pl.ANY)],
        out_specs=pl.BlockSpec(memory_space=pl.ANY),
        scratch_shapes=[pltpu.SemaphoreType.DMA((parts,))],
        compiler_params=pltpu.CompilerParams(vmem_limit_bytes=1 << 20),
        cost_estimate=pl.CostEstimate(
            flops=2 * pairs * parts * columns * 1024, bytes_accessed=4 * pairs * parts * columns, transcendentals=0
        ),
        name="lay",
    )(received)


def shards(fields, bracket, fraction):
    variables, _, rows, columns = fields.shape
    plev = bracket.shape[0]
    pairs = variables * plev
    lon_count, lat_count = lax.axis_size("lon"), lax.axis_size("lat")
    lon_place, lat_place = lax.axis_index("lon"), lax.axis_index("lat")
    assert rows == lon_count

    payload = interpolate(fields, bracket, fraction)
    received = lax.all_to_all(payload, "lon", split_axis=0, concat_axis=0, tiled=True)

    sums = jnp.sum(received[:, pairs:].astype(f32), 0)
    means = (sums[:rows] + sums[rows:]) / f32(lon_count * columns)
    first_place, last_place = lon_place == 0, lon_place == lon_count - 1

    edge = jnp.where(first_place, means[rows - 1], means[0])
    route = [(b, b + 1) for b in range(lat_count - 1)]
    along = [(0 * lat_count + s, 0 * lat_count + t) for s, t in route]
    along += [((lon_count - 1) * lat_count + t, (lon_count - 1) * lat_count + s) for s, t in route]
    beyond = lax.ppermute(edge, ("lon", "lat"), along)

    on_pressure = lay(received, pairs)

    own = lax.dynamic_index_in_dim(means, lon_place, 0, False)
    below = lax.dynamic_index_in_dim(means, jnp.maximum(lon_place - 1, 0), 0, False)
    above = lax.dynamic_index_in_dim(means, jnp.minimum(lon_place + 1, rows - 1), 0, False)
    below = jnp.where(first_place, beyond, below)
    above = jnp.where(last_place, beyond, above)
    first_row = first_place & (lat_place == 0)
    last_row = last_place & (lat_place == lat_count - 1)
    meridional = jnp.where(
        first_row, above - own, jnp.where(last_row, own - below, 0.5 * (above - below))
    )
    return (
        on_pressure.reshape(variables, plev, 1, lon_count * columns),
        own.reshape(variables, plev, 1),
        meridional.reshape(variables, plev, 1),
    )


def solution(mesh):
    return jax.shard_map(
        shards,
        mesh=mesh,
        in_specs=(P(None, None, "lat", "lon"), P(None, "lat", "lon"), P(None, "lat", "lon")),
        out_specs=(
            P(None, None, ("lat", "lon"), None),
            P(None, None, ("lat", "lon")),
            P(None, None, ("lat", "lon")),
        ),
        check_vma=False,
    )
```

profile of v0, /device:TPU:0, one launch (start us, length us, event | category | flops | bytes accessed | tf_op | source)
XLA Modules:
  0.0 21.5 jit_solution(7137193569955710121)
XLA Ops:
  0.6 2.8 %interpolate.1 = bf16[8,144,128]{2,1,0:T(8,128)(2,1)} custom-call(bf16[1,4,64,16,128]{4,3,2,1,0:T(8,128)(2,1)} %bitcast.29, s32[1,32,8,128]{3,2,1,0:T(8,128)} %bitcast.30, bf16[1,32,8,128]{3,2,1,0:T(8,128)(2,1)} %bitcast.31), custom_call_target="tpu_custom_call" | custom-call | tf_op jit(solution)/shard_map/interpolate/pallas_call | solution.py:73
  3.4 5.2 %all-to-all-start = ((bf16[8,144,128]{2,1,0:T(8,128)(2,1)}), bf16[8,144,128]{2,1,0:T(8,128)(2,1)S(1)}, u32[]{:S(2)}, u32[]{:S(2)}) async-start(bf16[8,144,128]{2,1,0:T(8,128)(2,1)} %interpolate.1), calls=%async_computation | async-start | bytes 589824 | tf_op jit(solution)/shard_map/all_to_all | solution.py:126
  8.6 7.3 %all-to-all-done.received = bf16[8,144,128]{2,1,0:T(8,128)(2,1)S(1)} async-done(((bf16[8,144,128]{2,1,0:T(8,128)(2,1)}), bf16[8,144,128]{2,1,0:T(8,128)(2,1)S(1)}, u32[]{:S(2)}, u32[]{:S(2)}) %all-to-all-start) | async-done | bytes 294944 | tf_op jit(solution)/shard_map/all_to_all | solution.py:126
  15.9 3.5 %collective-permute-start = (f32[128]{0:T(128)S(1)}, f32[128]{0:T(128)S(1)}, u32[]{:S(2)}, u32[]{:S(2)}) collective-permute-start(f32[128]{0:T(128)S(1)} %get-tuple-element.6), channel_id=1, source_target_pairs={{0,1},{1,2},{2,3},{29,28},{30,29},{31,30}} | collective-permute-start | bytes 1544 | tf_op jit(solution)/shard_map/ppermute | solution.py:136
  19.4 0.8 %lay.1 = bf16[128,1024]{1,0:T(8,128)(2,1)} custom-call(bf16[8,144,128]{2,1,0:T(8,128)(2,1)S(1)} %all-to-all-done.received), custom_call_target="tpu_custom_call" | custom-call | flops 268435456 | bytes 524288 | tf_op jit(solution)/shard_map/lay/pallas_call | solution.py:103
  20.2 0.7 %reshape.19 = f32[4,32,1]{1,0,2:T(4,128)} reshape(f32[128]{0:T(128)S(1)} %get-tuple-element.7) | data formatting | bytes 1024 | tf_op jit(solution)/shard_map/reshape | solution.py:152
  20.8 0.0 collective-permute-done
  20.9 0.7 %reshape.20 = f32[4,32,1]{1,0,2:T(4,128)} reshape(f32[128]{0:T(128)S(1)} %broadcast_select_fusion.4) | data formatting | bytes 1024 | tf_op jit(solution)/shard_map/reshape | solution.py:153
  (4 shorter events, 0.1 us)
Async XLA Ops:
  3.4 12.5 %all-to-all-start = ((bf16[8,144,128]{2,1,0:T(8,128)(2,1)}), bf16[8,144,128]{2,1,0:T(8,128)(2,1)S(1)}, u32[]{:S(2)}, u32[]{:S(2)}) async-start(bf16[8,144,128]{2,1,0:T(8,128)(2,1)} %interpolate.1), calls=%async_computation | async-start | bytes 589824 | tf_op jit(solution)/shard_map/all_to_all | solution.py:126
  15.9 4.9 %collective-permute-start = (f32[128]{0:T(128)S(1)}, f32[128]{0:T(128)S(1)}, u32[]{:S(2)}, u32[]{:S(2)}) collective-permute-start(f32[128]{0:T(128)S(1)} %get-tuple-element.6), channel_id=1, source_target_pairs={{0,1},{1,2},{2,3},{29,28},{30,29},{31,30}} | collective-permute-start | bytes 1544 | tf_op jit(solution)/shard_map/ppermute | solution.py:136
where the time goes:
time: 21.8 us; the launch traced here: 21.5 us
  starting transfers between devices  8.68 us (40%)
  waiting for transfers between devices  7.26 us (33%)
  Pallas kernels  3.55 us (16%)
  local copies, waits for them, and re-layouts  1.32 us (6%)
  between operations  0.66 us (3%)
    all_to_all x1, waiting for transfers between devices, shards(): lax.all_to_all(payload, 'lon', split_axis=0, concat_axis=0, tiled=True)  7.25 us
    all_to_all x1, starting transfers between devices, shards(): lax.all_to_all(payload, 'lon', split_axis=0, concat_axis=0, tiled=True)  5.2 us
    ppermute x1, starting transfers between devices, shards(): beyond = lax.ppermute(edge, ('lon', 'lat'), along)  3.48 us
    pallas_call x1, Pallas kernels, interpolate(): pl.pallas_call(functools.partial(interpolate_kernel, levels=levels), out_...  2.79 us
    pallas_call x1, Pallas kernels, lay(): pl.pallas_call(lay_kernel, out_shape=jax.ShapeDtypeStruct((pairs, parts *...  0.76 us
    reshape x1, local copies, waits for them, and re-layouts, shards(): meridional.reshape(variables, plev, 1)  0.66 us
    reshape x1, local copies, waits for them, and re-layouts, shards(): own.reshape(variables, plev, 1)  0.66 us
  transfers between devices with their start and end apart: 2, of which 1 were waited for; matrix products, arithmetic and copies ran while one was open for 3% of the time, Pallas kernels for 4%

commit v1 on v0

--- a/solution.py
+++ b/solution.py
@@ -129,11 +129,13 @@
     means = (sums[:rows] + sums[rows:]) / f32(lon_count * columns)
     first_place, last_place = lon_place == 0, lon_place == lon_count - 1
 
-    edge = jnp.where(first_place, means[rows - 1], means[0])
-    route = [(b, b + 1) for b in range(lat_count - 1)]
-    along = [(0 * lat_count + s, 0 * lat_count + t) for s, t in route]
-    along += [((lon_count - 1) * lat_count + t, (lon_count - 1) * lat_count + s) for s, t in route]
-    beyond = lax.ppermute(edge, ("lon", "lat"), along)
+    near = lon_place < lon_count // 2
+    edge = jnp.where(near, means[rows - 1], means[0])
+    ends = [((b, 0), (b - 1, 1)) for b in range(1, lat_count)]
+    ends += [((b, lon_count - 1), (b + 1, lon_count - 2)) for b in range(lat_count - 1)]
+    place = lambda at: at[1] * lat_count + at[0]
+    swaps = [(place(s), place(t)) for s, t in ends] + [(place(t), place(s)) for s, t in ends]
+    beyond = lax.ppermute(edge, ("lon", "lat"), swaps)
 
     on_pressure = lay(received, pairs)
 

time: 21.8 us -> 21.4 us (0.982)
  the two profiles are of different devices: /device:TPU:0 before, /device:TPU:1 now
where the time goes in v1:
time: 21.4 us; the launch traced here: 21.1 us
  starting transfers between devices  9.7 us (45%)
  waiting for transfers between devices  5.86 us (27%)
  Pallas kernels  3.55 us (17%)
  local copies, waits for them, and re-layouts  1.32 us (6%)
  between operations  0.66 us (3%)
    all_to_all x1, waiting for transfers between devices, shards(): lax.all_to_all(payload, 'lon', split_axis=0, concat_axis=0, tiled=True)  5.85 us
    all_to_all x1, starting transfers between devices, shards(): lax.all_to_all(payload, 'lon', split_axis=0, concat_axis=0, tiled=True)  5.21 us
    ppermute x1, starting transfers between devices, shards(): beyond = lax.ppermute(edge, ('lon', 'lat'), swaps)  4.49 us
    pallas_call x1, Pallas kernels, interpolate(): pl.pallas_call(functools.partial(interpolate_kernel, levels=levels), out_...  2.79 us
    pallas_call x1, Pallas kernels, lay(): pl.pallas_call(lay_kernel, out_shape=jax.ShapeDtypeStruct((pairs, parts *...  0.76 us
    reshape x1, local copies, waits for them, and re-layouts, shards(): meridional.reshape(variables, plev, 1)  0.66 us
    reshape x1, local copies, waits for them, and re-layouts, shards(): own.reshape(variables, plev, 1)  0.66 us
  transfers between devices with their start and end apart: 2, of which 1 were waited for; matrix products, arithmetic and copies ran while one was open for 3% of the time, Pallas kernels for 4%

profile of v1, /device:TPU:1, one launch (start us, length us, event | category | flops | bytes accessed | tf_op | source)
XLA Modules:
  0.0 21.1 jit_solution(319247272427010223)
XLA Ops:
  0.6 2.8 %interpolate.1 = bf16[8,144,128]{2,1,0:T(8,128)(2,1)} custom-call(bf16[1,4,64,16,128]{4,3,2,1,0:T(8,128)(2,1)} %bitcast.29, s32[1,32,8,128]{3,2,1,0:T(8,128)} %bitcast.30, bf16[1,32,8,128]{3,2,1,0:T(8,128)(2,1)} %bitcast.31), custom_call_target="tpu_custom_call" | custom-call | tf_op jit(solution)/shard_map/interpolate/pallas_call | solution.py:73
  3.4 5.2 %all-to-all-start = ((bf16[8,144,128]{2,1,0:T(8,128)(2,1)}), bf16[8,144,128]{2,1,0:T(8,128)(2,1)S(1)}, u32[]{:S(2)}, u32[]{:S(2)}) async-start(bf16[8,144,128]{2,1,0:T(8,128)(2,1)} %interpolate.1), calls=%async_computation | async-start | bytes 589824 | tf_op jit(solution)/shard_map/all_to_all | solution.py:126
  8.6 5.9 %all-to-all-done.received = bf16[8,144,128]{2,1,0:T(8,128)(2,1)S(1)} async-done(((bf16[8,144,128]{2,1,0:T(8,128)(2,1)}), bf16[8,144,128]{2,1,0:T(8,128)(2,1)S(1)}, u32[]{:S(2)}, u32[]{:S(2)}) %all-to-all-start) | async-done | bytes 294944 | tf_op jit(solution)/shard_map/all_to_all | solution.py:126
  14.5 4.5 %collective-permute-start = (f32[128]{0:T(128)S(1)}, f32[128]{0:T(128)S(1)}, u32[]{:S(2)}, u32[]{:S(2)}) collective-permute-start(f32[128]{0:T(128)S(1)} %get-tuple-element.6), channel_id=1, source_target_pairs={{1,4},{2,5},{3,6},{28,25},{29,26},{30,27},{4,1},{5,2},{6,3},{25,28... | collective-permute-start | bytes 1544 | tf_op jit(solution)/shard_map/ppermute | solution.py:138
  19.0 0.8 %lay.1 = bf16[128,1024]{1,0:T(8,128)(2,1)} custom-call(bf16[8,144,128]{2,1,0:T(8,128)(2,1)S(1)} %all-to-all-done.received), custom_call_target="tpu_custom_call" | custom-call | flops 268435456 | bytes 524288 | tf_op jit(solution)/shard_map/lay/pallas_call | solution.py:103
  19.8 0.7 %reshape.19 = f32[4,32,1]{1,0,2:T(4,128)} reshape(f32[128]{0:T(128)S(1)} %get-tuple-element.7) | data formatting | bytes 1024 | tf_op jit(solution)/shard_map/reshape | solution.py:154
  20.5 0.0 collective-permute-done
  20.5 0.7 %reshape.20 = f32[4,32,1]{1,0,2:T(4,128)} reshape(f32[128]{0:T(128)S(1)} %broadcast_select_fusion.4) | data formatting | bytes 1024 | tf_op jit(solution)/shard_map/reshape | solution.py:155
  (4 shorter events, 0.1 us)
Async XLA Ops:
  3.4 11.1 %all-to-all-start = ((bf16[8,144,128]{2,1,0:T(8,128)(2,1)}), bf16[8,144,128]{2,1,0:T(8,128)(2,1)S(1)}, u32[]{:S(2)}, u32[]{:S(2)}) async-start(bf16[8,144,128]{2,1,0:T(8,128)(2,1)} %interpolate.1), calls=%async_computation | async-start | bytes 589824 | tf_op jit(solution)/shard_map/all_to_all | solution.py:126
  14.5 5.9 %collective-permute-start = (f32[128]{0:T(128)S(1)}, f32[128]{0:T(128)S(1)}, u32[]{:S(2)}, u32[]{:S(2)}) collective-permute-start(f32[128]{0:T(128)S(1)} %get-tuple-element.6), channel_id=1, source_target_pairs={{1,4},{2,5},{3,6},{28,25},{29,26},{30,27},{4,1},{5,2},{6,3},{25,28... | collective-permute-start | bytes 1544 | tf_op jit(solution)/shard_map/ppermute | solution.py:138
